TPU v7x, 32 devices: a whole 2x2x4 slice. The times are simulated.
32 devices in a mesh: group: 4 (over z), member: 8 (over y, x, core).
Axes of the slice: x: 2, y: 2, z: 4, core: 2. Of those that a mesh axis runs over, the one named last changes fastest.
Arguments:
- hidden: bfloat16 [6144, 2048], P('group'), may hold values from -6 to 6
- token_slab: int32 [6144, 1], P(('group', 'member')), may hold values from 0 to 31; in each aligned block of 192 rows (0 to 191, 192 to 383, ...) at most 12 rows name the same one
- token_row: int32 [6144], P(('group', 'member')), may hold values from 0 to 8191
- slab_owner: int32 [32], replicated, may hold values from 0 to 31, each once
- ple_table: bfloat16 [262144, 256], P(('group', 'member')), may hold values from -0.375 to 0.375
- norm_gains: float32 [1, 3, 2048], replicated, may hold values from 0.1 to 1.9
- w_gate: bfloat16 [1, 2048, 8192], P(None, None, 'member'), may hold values from -0.125 to 0.125
- w_up: bfloat16 [1, 2048, 8192], P(None, None, 'member'), may hold values from -0.125 to 0.125
- w_down: bfloat16 [1, 8192, 2048], P(None, 'member'), may hold values from -0.0625 to 0.0625
- ple_gate: bfloat16 [1, 2048, 256], P(None, None, 'member'), may hold values from -0.125 to 0.125
- ple_proj: bfloat16 [1, 256, 2048], P(None, 'member'), may hold values from -0.375 to 0.375
Outputs:
- hidden_out: bfloat16 [6144, 2048], P('group')
Inputs may be any that keep to these rules, and one draw needn't show every extreme that they name: Within the 192 tokens of one device (aligned blocks of token_slab), no slab is named by more than 12 tokens. Each number appears once: slab s is stored in rows slab_owner[s] * 8192 to slab_owner[s] * 8192 + 8191 of ple_table.
All inputs are finite; a program needn't handle non-finite values.
Results may differ from a plain program's by a relative error of at most 0.0061.
Values may be sent and summed in bfloat16 or wider, within the bound.
No kernel may reach another device: no remote copies, remote signals or barrier semaphores. Data moves between devices by JAX's collectives and lax.ppermute only.
A program may use at most 128 MiB of HBM per device.

v0:
```python
import jax
import jax.numpy as jnp
from jax import lax
from jax.sharding import PartitionSpec as P

PLE = 256
epsilon = 1e-06


def norm_rows(values, scales):
    return values * lax.rsqrt(jnp.mean(values * values, axis=-1, keepdims=True) + epsilon) * scales


def lookup_rows(wanted, ple_table):
    flat_ids = wanted.reshape(-1) - 1
    one_hot = (
        flat_ids[:, None] == jnp.arange(ple_table.shape[0], dtype=jnp.int32)[None, :]
    ).astype(jnp.bfloat16)
    served = jnp.dot(one_hot, ple_table, preferred_element_type=jnp.float32).astype(jnp.bfloat16)
    return served.reshape(wanted.shape + (ple_table.shape[1],))


def request_slots(slab_ids, token_row, slab_owner, devices, slots):
    target = slab_owner[slab_ids]
    order = jnp.arange(token_row.shape[0], dtype=jnp.int32)
    earlier = (target[None, :] == target[:, None]) & (order[None, :] < order[:, None])
    slot_of = jnp.sum(earlier.astype(jnp.int32), axis=1)
    hit_map = (target[:, None, None] == jnp.arange(devices, dtype=jnp.int32)[None, :, None]) & (
        slot_of[:, None, None] == jnp.arange(slots, dtype=jnp.int32)[None, None, :]
    )
    requests = jnp.sum(jnp.where(hit_map, token_row[:, None, None] + 1, 0), axis=0)
    return (hit_map, requests)


def pick_rows(hit_map, returned):
    return jnp.einsum(
        "tdc,dcw->tw", hit_map.astype(jnp.bfloat16), returned, preferred_element_type=jnp.float32
    ).astype(jnp.bfloat16)


def combine_branch(current, partial_value, scales):
    share = lax.psum_scatter(partial_value, "member", scatter_dimension=1, tiled=True)
    share_width = share.shape[1]
    offset = lax.axis_index("member") * share_width
    squares = lax.psum(jnp.sum(share * share, axis=-1, keepdims=True), "member")
    normed = (
        share
        * lax.rsqrt(squares / (share_width * lax.axis_size("member")) + epsilon)
        * lax.dynamic_slice_in_dim(scales, offset, share_width, 0)
    )
    updated = lax.dynamic_slice_in_dim(current, offset, share_width, 1) + normed
    return lax.all_gather(updated, "member", axis=1, tiled=True)


def per_device(
    hidden,
    token_slab,
    token_row,
    slab_owner,
    ple_table,
    norm_gains,
    w_gate,
    w_up,
    w_down,
    ple_gate,
    ple_proj,
):
    members = lax.axis_size("member")
    devices = lax.axis_size("group") * members
    tokens_here = token_row.shape[0]
    slots = max(2, (2 * tokens_here + devices - 1) // devices)
    slab_ids = token_slab[:, 0]
    hit_map, requests = request_slots(slab_ids, token_row, slab_owner, devices, slots)
    grouped = requests.reshape(lax.axis_size("group"), members, slots)
    received = lax.all_to_all(
        lax.all_to_all(grouped, "group", split_axis=0, concat_axis=0, tiled=True),
        "member",
        split_axis=1,
        concat_axis=1,
        tiled=True,
    )
    served = lookup_rows(received, ple_table)
    returned = lax.all_to_all(
        lax.all_to_all(served, "group", split_axis=0, concat_axis=0, tiled=True),
        "member",
        split_axis=1,
        concat_axis=1,
        tiled=True,
    )
    own_rows = pick_rows(hit_map, returned.reshape(devices, slots, ple_table.shape[1]))
    per_member = ple_gate.shape[2]
    layers = w_gate.shape[0]
    pieces = own_rows.reshape(tokens_here, layers, members, per_member)
    columns = lax.all_to_all(pieces, "member", split_axis=2, concat_axis=0, tiled=True)
    ple_part = columns.reshape(-1, layers, per_member).astype(jnp.float32) * PLE**0.5
    current = hidden.astype(jnp.float32)
    normed = norm_rows(current, norm_gains[0, 0]).astype(jnp.bfloat16)
    gate_part = jnp.dot(normed, w_gate[0], preferred_element_type=jnp.float32)
    up_part = jnp.dot(normed, w_up[0], preferred_element_type=jnp.float32)
    activated = (jax.nn.gelu(gate_part, approximate=True) * up_part).astype(jnp.bfloat16)
    mlp_out = jnp.dot(activated, w_down[0], preferred_element_type=jnp.float32)
    current = combine_branch(current, mlp_out, norm_gains[0, 1])
    current_b = current.astype(jnp.bfloat16)
    ple_gate_out = jnp.dot(current_b, ple_gate[0], preferred_element_type=jnp.float32)
    ple_act = (jax.nn.gelu(ple_gate_out, approximate=True) * ple_part[:, 0, :]).astype(jnp.bfloat16)
    ple_out = jnp.dot(ple_act, ple_proj[0], preferred_element_type=jnp.float32)
    current = combine_branch(current, ple_out, norm_gains[0, 2])
    return current.astype(jnp.bfloat16)


def solution(mesh):
    return jax.shard_map(
        per_device,
        mesh=mesh,
        in_specs=(
            P("group", None),
            P(("group", "member"), None),
            P(("group", "member")),
            P(),
            P(("group", "member"), None),
            P(),
            P(None, None, "member"),
            P(None, None, "member"),
            P(None, "member", None),
            P(None, None, "member"),
            P(None, "member", None),
        ),
        out_specs=P("group", None),
        check_vma=False,
    )
```

profile of v0, /device:TPU:0, one launch (start us, length us, event | category | flops | bytes accessed | tf_op | source)
XLA Modules:
  0.0 417.3 jit_solution(211991118664863560)
XLA Ops:
  6.5 4.2 %multiply_reduce_fusion = f32[1536]{0:T(1024)S(1)} fusion(bf16[1536,2048]{1,0:T(8,128)(2,1)} %param.11), kind=kLoop, calls=%fused_computation.2 | loop fusion | flops 9435648 | bytes 6297600 | tf_op jit(solution)/shard_map/reduce_sum | solution.py:11
  10.8 0.4 copy-done.1
  11.2 10.4 %fusion.17 = f32[1536,1024]{1,0:T(8,128)} fusion(bf16[1,2048,1024]{2,1,0:T(8,128)(2,1)} %param.17, f32[2048]{0:T(1024)S(1)} %bitcast.75, f32[1536]{0:T(1024)S(1)} %add_rsqrt_fusion, bf16[1536,2048]{1,0:T(8,128)(2,1)S(1)} %copy-done.1), kind=kOutput, calls=%fused_computation.20 | convolution fusion | flops 6455033856 | bytes 16791552 | tf_op jit(solution)/shard_map/dot_general | solution.py:98
  21.6 22.6 %fusion.13 = f32[1536,2048]{1,0:T(8,128)} fusion(bf16[1,1024,2048]{2,1,0:T(8,128)(2,1)} %param.19, f32[1536,1024]{1,0:T(8,128)} %fusion.17, bf16[1,2048,1024]{2,1,0:T(8,128)(2,1)} %param.18, f32[2048]{0:T(1024)S(1)} %bitcast.76, f32[1536]{0:T(1024)S(1)} %add_rsqrt_fusion, bf16[1536,2048]{1,0:T(8,128)(2,1)} %param.11), kind=kOutput, calls=%fused_computation.17 | convolution fusion | flops 12913213440 | bytes 33568768 | tf_op jit(solution)/shard_map/dot_general | solution.py:101
  44.2 0.2 all-gather.3.cloned.1.call-start
  44.5 9.5 %convert_element_type.38 = f32[1536,2048]{1,0:T(8,128)} convert(bf16[1536,2048]{1,0:T(8,128)(2,1)} %param.11) | non-fusion elementwise | flops 3145728 | bytes 18874368 | tf_op jit(solution)/shard_map/convert_element_type | solution.py:96
  54.0 85.1 %reduce-scatter.3.cloned.1.call-done = f32[1536,256]{1,0:T(8,128)} async-done(((f32[1536,2048]{1,0:T(8,128)}), f32[1536,256]{1,0:T(8,128)}) %reduce-scatter.3.cloned.1.call-update) | async-done | bytes 1572880 | tf_op jit(solution)/shard_map/reduce_scatter | solution.py:42
  139.1 1.7 multiply_reduce_fusion.2
  140.8 12.8 %psum.14 = f32[1536,1]{0,1:T(1,128)S(1)} all-reduce(f32[1536,1]{0,1:T(1,128)S(1)} %broadcast_in_dim.12), channel_id=1, replica_groups=mesh['group'=4,'member'=8] {'member'}, use_global_device_ids=true, to_apply=%region_3.4 | all-reduce | flops 1536 | bytes 12288 | tf_op jit(solution)/shard_map/psum | solution.py:45
  153.6 3.3 multiply_add_fusion.1
  157.0 0.7 fusion.67
  157.7 0.7 fusion.66
  158.4 4.3 %compare_select_fusion.1 = (s32[192,1]{0,1:T(1,128)S(1)}, s32[192,1]{0,1:T(1,128)S(1)}) fusion(s32[]{:T(128)} %bitcast.31, s32[]{:T(128)} %bitcast.32, s32[]{:T(128)} %bitcast.33, s32[]{:T(128)} %bitcast.34, s32[]{:T(128)} %bitcast.35, s32[]{:T(128)} %bitcast.37, s32[]{:T(128)} %bitcast.36, s32[192,1]{0,1:T(1,128)S(1)} %copy-done.6), kind=kLoop, calls=%fused_computation.93 | loop fusion | flops 2880 | bytes 2332 | tf_op jit(solution)/shard_map/gather | solution.py:24
  162.8 15.6 %select_select_fusion = s32[192]{0:T(256)S(1)} fusion(pred[192]{0:T(512)(128)(4,1)S(1)} %get-tuple-element.29, pred[192]{0:T(512)(128)(4,1)S(1)} %get-tuple-element.28, pred[192]{0:T(512)(128)(4,1)S(1)} %get-tuple-element.27, pred[192]{0:T(512)(128)(4,1)S(1)} %get-tuple-element.26, pred[192]{0:T(512)(128)(4,1)S(1)} %get-tuple-element.25, ...), kind=kLoop, calls=%fused_computation.99 | loop fusion | flops 4800 | bytes 6436 | tf_op jit(solution)/shard_map/gather | solution.py:24
  178.4 0.2 convert_reduce_fusion
  178.7 0.3 fusion.26
  179.1 10.0 %all_to_all.29 = s32[4,8,12]{2,1,0:T(8,128)S(1)} all-to-all(s32[4,8,12]{2,1,0:T(8,128)S(1)} %bitcast.74), channel_id=1, replica_groups=mesh['group'=4,'member'=8] {'group'}, dimensions={0} | all-to-all | bytes 3072 | tf_op jit(solution)/shard_map/all_to_all | solution.py:76
  189.0 7.6 %all_to_all.30 = s32[4,8,12]{2,0,1:T(4,128)S(1)} all-to-all(s32[4,8,12]{2,0,1:T(4,128)S(1)} %copy.43), channel_id=1, replica_groups=mesh['group'=4,'member'=8] {'member'}, dimensions={1} | all-to-all | bytes 3072 | tf_op jit(solution)/shard_map/all_to_all | solution.py:75
  196.8 4.6 %fusion.23 = bf16[384,256]{1,0:T(8,128)(2,1)S(1)} fusion(bf16[8192,256]{1,0:T(8,128)(2,1)} %param.15, s32[384]{0:T(512)S(1)} %sub.7), kind=kOutput, calls=%fused_computation.30 | convolution fusion | flops 1613856768 | bytes 4392448 | tf_op jit(solution)/shard_map/dot_general | solution.py:19
  201.5 10.0 %all_to_all.31 = bf16[4,8,12,256]{3,1,2,0:T(8,128)(2,1)S(1)} all-to-all(bf16[4,8,12,256]{3,1,2,0:T(8,128)(2,1)S(1)} %copy.45), channel_id=1, replica_groups=mesh['group'=4,'member'=8] {'group'}, dimensions={0} | all-to-all | bytes 393216 | tf_op jit(solution)/shard_map/all_to_all | solution.py:84
  211.7 11.1 %all_to_all.32 = bf16[4,8,12,256]{3,0,2,1:T(4,128)(2,1)S(1)} all-to-all(bf16[4,8,12,256]{3,0,2,1:T(4,128)(2,1)S(1)} %copy.46), channel_id=1, replica_groups=mesh['group'=4,'member'=8] {'member'}, dimensions={1} | all-to-all | bytes 393216 | tf_op jit(solution)/shard_map/all_to_all | solution.py:83
  222.8 0.3 fusion.24
  223.2 8.2 %all_to_all.33 = bf16[192,1,8,32]{0,3,1,2:T(8,128)(2,1)S(1)} all-to-all(bf16[192,1,8,32]{0,3,1,2:T(8,128)(2,1)S(1)} %bitcast.73), channel_id=1, replica_groups=mesh['group'=4,'member'=8] {'member'}, dimensions={2} | all-to-all | bytes 196608 | tf_op jit(solution)/shard_map/all_to_all | solution.py:94
  231.4 0.2 copy.50
  231.7 2.3 all-gather.3.cloned.1.call-done
  234.0 12.7 %fusion.43 = f32[1536,2048]{1,0:T(8,128)} fusion(f32[1536,32]{0,1:T(8,128)S(1)} %mul.170, f32[1536,2048]{1,0:T(8,128)} %all-gather.3.cloned.1.call-done, bf16[1,32,2048]{2,1,0:T(8,128)(2,1)S(1)} %copy-done, bf16[1,2048,32]{1,2,0:T(8,128)(2,1)S(1)} %copy-done.3), kind=kOutput, calls=%fused_computation.47 | convolution fusion | flops 406290432 | bytes 25624576 | tf_op jit(solution)/shard_map/dot_general | solution.py:106
  246.8 93.1 %reduce-scatter.5.cloned.1.call-done = f32[1536,256]{1,0:T(8,128)} async-done(((f32[1536,2048]{1,0:T(8,128)}), f32[1536,256]{1,0:T(8,128)}) %reduce-scatter.5.cloned.1.call-update) | async-done | bytes 1572880 | tf_op jit(solution)/shard_map/reduce_scatter | solution.py:42
  339.8 1.7 multiply_reduce_fusion.1
  341.5 12.8 %psum.15 = f32[1536,1]{0,1:T(1,128)S(1)} all-reduce(f32[1536,1]{0,1:T(1,128)S(1)} %broadcast_in_dim.19), channel_id=1, replica_groups=mesh['group'=4,'member'=8] {'member'}, use_global_device_ids=true, to_apply=%region_8.9 | all-reduce | flops 1536 | bytes 12288 | tf_op jit(solution)/shard_map/psum | solution.py:45
  354.4 3.0 multiply_add_fusion
  357.4 46.7 %all-gather.5.cloned.1.call-done = bf16[1536,2048]{1,0:T(8,128)(2,1)} async-done(((bf16[1536,256]{1,0:T(8,128)(2,1)}), bf16[1536,2048]{1,0:T(8,128)(2,1)}) %all-gather.5.cloned.1.call-update) | async-done | bytes 6291472 | tf_op jit(solution)/shard_map/all_gather | solution.py:52
  404.1 6.6 %copy.57 = bf16[1536,2048]{1,0:T(8,128)(2,1)} copy(bf16[1536,2048]{1,0:T(8,128)(2,1)} %all-gather.5.cloned.1.call-done) | data formatting | bytes 12582912
  (42 shorter events, 1.1 us)
Async XLA Ops:
  6.5 227.5 %copy-start = (bf16[1,32,2048]{2,1,0:T(8,128)(2,1)S(1)}, bf16[1,32,2048]{2,1,0:T(8,128)(2,1)}, u32[]{:S(2)}) copy-start(bf16[1,32,2048]{2,1,0:T(8,128)(2,1)} %param.21) | copy-start | bytes 393220
  6.5 4.3 %copy-start.4 = (f32[1,3,2048]{2,0,1:T(1,128)S(1)}, f32[1,3,2048]{2,0,1:T(1,128)}, u32[]{:S(2)}) copy-start(f32[1,3,2048]{2,0,1:T(1,128)} %param.16) | copy-start | bytes 73732
  6.5 132.5 %reduce-scatter.3.cloned.1.call-start = ((), (), s32[]{:S(2)}) async-start(), calls=%async_computation.7 | async-start | bytes 14155776 | tf_op jit(solution)/shard_map/reduce_scatter | solution.py:42
  6.5 4.6 %copy-start.1 = (bf16[1536,2048]{1,0:T(8,128)(2,1)S(1)}, bf16[1536,2048]{1,0:T(8,128)(2,1)}, u32[]{:S(2)}) copy-start(bf16[1536,2048]{1,0:T(8,128)(2,1)} %param.11) | copy-start | bytes 18874372
  44.2 189.8 %all-gather.3.cloned.1.call-start = ((), (), s32[]{:S(2)}) async-start(), calls=%async_computation.8 | async-start | bytes 14155776 | tf_op jit(solution)/shard_map/all_gather | solution.py:52
  54.0 103.0 %copy-start.2 = (s32[32]{0:T(128)S(1)}, s32[32]{0:T(128)}, u32[]{:S(2)}) copy-start(s32[32]{0:T(128)} %param.14) | copy-start | bytes 388
  54.0 104.4 %copy-start.6 = (s32[192,1]{0,1:T(1,128)S(1)}, s32[192,1]{0,1:T(1,128)}, u32[]{:S(2)}) copy-start(s32[192,1]{0,1:T(1,128)} %param.12) | copy-start | bytes 2308
  54.0 124.6 %copy-start.5 = (s32[192]{0:T(256)S(1)}, s32[192]{0:T(256)}, u32[]{:S(2)}) copy-start(s32[192]{0:T(256)} %param.13) | copy-start | bytes 2308
  156.9 182.9 %reduce-scatter.5.cloned.1.call-start = ((), (), s32[]{:S(2)}) async-start(), calls=%async_computation.9 | async-start | bytes 14155776 | tf_op jit(solution)/shard_map/reduce_scatter | solution.py:42
  196.8 37.2 %copy-start.3 = (bf16[1,2048,32]{1,2,0:T(8,128)(2,1)S(1)}, bf16[1,2048,32]{1,2,0:T(8,128)(2,1)}, u32[]{:S(2)}) copy-start(bf16[1,2048,32]{1,2,0:T(8,128)(2,1)} %param.20) | copy-start | bytes 393220
  246.7 157.4 %all-gather.5.cloned.1.call-start = ((), (), s32[]{:S(2)}) async-start(), calls=%async_computation.10 | async-start | bytes 7077888 | tf_op jit(solution)/shard_map/all_gather | solution.py:52
Sparse Core Ops, SparseCore 0:
  44.4 94.6 reduce-scatter.2
  157.0 76.9 all-gather.2
  246.8 92.9 reduce-scatter.4
  357.5 46.5 all-gather.4
where the time goes:
time: 418 us; the launch traced here: 417 us
  waiting for transfers between devices  227 us (54%)
  blocking collectives  72.4 us (17%)
  matrix products  50.5 us (12%)
  other arithmetic  44 us (11%)
  between operations  13.4 us (3%)
  local copies, waits for them, and re-layouts  9.3 us (2%)
    reduce_scatter x2, waiting for transfers between devices, combine_branch(): lax.psum_scatter(partial_value, 'member', scatter_dimension=1, tiled=True)  178 us
    all_gather x2, waiting for transfers between devices, combine_branch(): return lax.all_gather(updated, 'member', axis=1, tiled=True)  49.1 us
    psum x2, blocking collectives, combine_branch(): squares = lax.psum(jnp.sum(share * share, axis=-1, keepdims=True), 'member')  25.5 us
    dot_general x1, matrix products, per_device(): mlp_out = jnp.dot(activated, w_down[0], preferred_element_type=jnp.float32)  22.6 us
    gather x3, other arithmetic, request_slots(): target = slab_owner[slab_ids]  20 us
    dot_general x1, matrix products, per_device(): ple_out = jnp.dot(ple_act, ple_proj[0], preferred_element_type=jnp.float32)  12.7 us
    all_to_all x1, blocking collectives, per_device(): lax.all_to_all(lax.all_to_all(served, 'group', split_axis=0, concat_axis=...  11.1 us
    dot_general x1, matrix products, per_device(): gate_part = jnp.dot(normed, w_gate[0], preferred_element_type=jnp.float32)  10.4 us
  transfers between devices with their start and end apart: 4, of which 4 were waited for; matrix products, arithmetic and copies ran while one was open for 9% of the time, Pallas kernels for 0%

commit v1 on v0

--- a/solution.py
+++ b/solution.py
@@ -49,7 +49,9 @@
         * lax.dynamic_slice_in_dim(scales, offset, share_width, 0)
     )
     updated = lax.dynamic_slice_in_dim(current, offset, share_width, 1) + normed
-    return lax.all_gather(updated, "member", axis=1, tiled=True)
+    return jnp.concatenate(
+        lax.all_to_all(jnp.stack([updated] * lax.axis_size("member")), "member", 0, 0), axis=1
+    )
 
 
 def per_device(

time: 418 us -> 537 us (1.28)
  blocking collectives: 72.4 us -> 131 us
  local copies, waits for them, and re-layouts: 9.3 us -> 53 us
  starting transfers between devices: 0.31 us -> 13 us
  waiting for transfers between devices: 227 us -> 236 us
    all_to_all x0 -> x3, waiting for transfers between devices: none -> 139 us  [the longest x1 139 us: combine_branch(): lax.all_to_all(jnp.stack([updated] * lax.axis_size('member')), 'member',...]
    reduce_scatter x2, waiting for transfers between devices: 178 us -> 97.5 us  [combine_branch(): lax.psum_scatter(partial_value, 'member', scatter_dimension=1, tiled=True)]
    all_to_all x2 -> x1, blocking collectives: 19.3 us -> 74.9 us  [combine_branch(): lax.all_to_all(jnp.stack([updated] * lax.axis_size('member')), 'member',...]
    all_gather x2 -> x0, waiting for transfers between devices: 49.1 us -> none  [combine_branch(): return lax.all_gather(updated, 'member', axis=1, tiled=True)]
    all_to_all x0 -> x2, local copies, waits for them, and re-layouts: none -> 18.6 us  [combine_branch(): lax.all_to_all(jnp.stack([updated] * lax.axis_size('member')), 'member',...]
    reshape x0 -> x1, local copies, waits for them, and re-layouts: none -> 15.2 us  [combine_branch(): jnp.concatenate(lax.all_to_all(jnp.stack([updated] * lax.axis_size('membe...]
    all_to_all x0 -> x3, starting transfers between devices: none -> 13 us  [the longest x1 5.34 us: combine_branch(): lax.all_to_all(jnp.stack([updated] * lax.axis_size('member')), 'member',...]
    convert_element_type x0 -> x1, local copies, waits for them, and re-layouts: none -> 8.61 us  [per_device(): return current.astype(jnp.bfloat16)]
  transfers between devices with their start and end apart: 4 -> 5, of which waited for: 4 -> 3; matrix products, arithmetic and copies ran while one was open for 9% -> 11% of each run, Pallas kernels for 0% -> 0%
where the time goes in v1:
time: 537 us; the launch traced here: 536 us
  waiting for transfers between devices  236 us (44%)
  blocking collectives  131 us (24%)
  local copies, waits for them, and re-layouts  53 us (10%)
  matrix products  48 us (9%)
  other arithmetic  41.4 us (8%)
  between operations  13.7 us (3%)
  starting transfers between devices  13 us (2%)
    all_to_all x1, waiting for transfers between devices, combine_branch(): lax.all_to_all(jnp.stack([updated] * lax.axis_size('member')), 'member',...  139 us
    reduce_scatter x2, waiting for transfers between devices, combine_branch(): lax.psum_scatter(partial_value, 'member', scatter_dimension=1, tiled=True)  97.5 us
    all_to_all x1, blocking collectives, combine_branch(): lax.all_to_all(jnp.stack([updated] * lax.axis_size('member')), 'member',...  74.9 us
    psum x2, blocking collectives, combine_branch(): squares = lax.psum(jnp.sum(share * share, axis=-1, keepdims=True), 'member')  25.5 us
    dot_general x1, matrix products, per_device(): mlp_out = jnp.dot(activated, w_down[0], preferred_element_type=jnp.float32)  22.6 us
    gather x3, other arithmetic, request_slots(): target = slab_owner[slab_ids]  20.1 us
    all_to_all x2, local copies, waits for them, and re-layouts, combine_branch(): lax.all_to_all(jnp.stack([updated] * lax.axis_size('member')), 'member',...  18.6 us
    reshape x1, local copies, waits for them, and re-layouts, combine_branch(): jnp.concatenate(lax.all_to_all(jnp.stack([updated] * lax.axis_size('membe...  15.2 us
  transfers between devices with their start and end apart: 5, of which 3 were waited for; matrix products, arithmetic and copies ran while one was open for 11% of the time, Pallas kernels for 0%

profile of v1, /device:TPU:0, one launch (start us, length us, event | category | flops | bytes accessed | tf_op | source)
XLA Modules:
  0.0 535.8 jit_solution(17045676051018718924)
XLA Ops:
  6.5 4.2 multiply_reduce_fusion
  11.2 10.4 %fusion.15 = f32[1536,1024]{1,0:T(8,128)} fusion(bf16[1,2048,1024]{2,1,0:T(8,128)(2,1)} %param.17, f32[2048]{0:T(1024)S(1)} %bitcast.91, f32[1536]{0:T(1024)S(1)} %add_rsqrt_fusion, bf16[1536,2048]{1,0:T(8,128)(2,1)S(1)} %copy-done.1), kind=kOutput, calls=%fused_computation.19 | convolution fusion | flops 6455033856 | bytes 16791552 | tf_op jit(solution)/shard_map/dot_general | solution.py:100
  21.6 22.6 %fusion.11 = f32[1536,2048]{1,0:T(8,128)} fusion(bf16[1,1024,2048]{2,1,0:T(8,128)(2,1)} %param.19, f32[1536,1024]{1,0:T(8,128)} %fusion.15, bf16[1,2048,1024]{2,1,0:T(8,128)(2,1)} %param.18, f32[2048]{0:T(1024)S(1)} %bitcast.92, f32[1536]{0:T(1024)S(1)} %add_rsqrt_fusion, bf16[1536,2048]{1,0:T(8,128)(2,1)} %param.11), kind=kOutput, calls=%fused_computation.16 | convolution fusion | flops 12913213440 | bytes 33568768 | tf_op jit(solution)/shard_map/dot_general | solution.py:103
  45.6 0.7 fusion.60
  46.3 4.3 compare_select_fusion.1
  50.7 15.6 %select_select_fusion = s32[192]{0:T(256)S(1)} fusion(pred[192]{0:T(512)(128)(4,1)S(1)} %get-tuple-element.29, pred[192]{0:T(512)(128)(4,1)S(1)} %get-tuple-element.28, pred[192]{0:T(512)(128)(4,1)S(1)} %get-tuple-element.27, pred[192]{0:T(512)(128)(4,1)S(1)} %get-tuple-element.26, pred[192]{0:T(512)(128)(4,1)S(1)} %get-tuple-element.25, ...), kind=kLoop, calls=%fused_computation.99 | loop fusion | flops 4800 | bytes 6436 | tf_op jit(solution)/shard_map/gather | solution.py:24
  67.0 11.7 %all_to_all.39 = s32[4,8,12]{2,1,0:T(8,128)S(1)} all-to-all(s32[4,8,12]{2,1,0:T(8,128)S(1)} %bitcast.90), channel_id=1, replica_groups=mesh['group'=4,'member'=8] {'group'}, dimensions={0} | all-to-all | bytes 3072 | tf_op jit(solution)/shard_map/all_to_all | solution.py:78
  78.8 8.6 %all_to_all.40 = s32[4,8,12]{2,0,1:T(4,128)S(1)} all-to-all(s32[4,8,12]{2,0,1:T(4,128)S(1)} %copy.54), channel_id=1, replica_groups=mesh['group'=4,'member'=8] {'member'}, dimensions={1} | all-to-all | bytes 3072 | tf_op jit(solution)/shard_map/all_to_all | solution.py:77
  87.4 4.7 fusion.21
  92.3 9.8 %all_to_all.41 = bf16[4,8,12,256]{3,1,2,0:T(8,128)(2,1)S(1)} all-to-all(bf16[4,8,12,256]{3,1,2,0:T(8,128)(2,1)S(1)} %copy.56), channel_id=1, replica_groups=mesh['group'=4,'member'=8] {'group'}, dimensions={0} | all-to-all | bytes 393216 | tf_op jit(solution)/shard_map/all_to_all | solution.py:86
  102.1 0.8 copy.57
  103.0 3.4 all-to-all-start.4
  106.4 8.8 %convert_element_type.47 = f32[1536,2048]{1,0:T(8,128)} convert(bf16[1536,2048]{1,0:T(8,128)(2,1)} %param.11) | non-fusion elementwise | flops 3145728 | bytes 18874368 | tf_op jit(solution)/shard_map/convert_element_type | solution.py:98
  115.4 0.8 copy.59
  116.2 4.3 all-to-all-start.5
  120.4 22.3 %reduce-scatter.3.cloned.1.call-done = f32[1536,256]{1,0:T(8,128)} async-done(((f32[1536,2048]{1,0:T(8,128)}), f32[1536,256]{1,0:T(8,128)}) %reduce-scatter.3.cloned.1.call-update) | async-done | bytes 1572880 | tf_op jit(solution)/shard_map/reduce_scatter | solution.py:42
  142.8 1.7 multiply_reduce_fusion.2
  144.5 12.8 %psum.14 = f32[1536,1]{0,1:T(1,128)S(1)} all-reduce(f32[1536,1]{0,1:T(1,128)S(1)} %broadcast_in_dim.12), channel_id=1, replica_groups=mesh['group'=4,'member'=8] {'member'}, use_global_device_ids=true, to_apply=%region_3.4 | all-reduce | flops 1536 | bytes 12288 | tf_op jit(solution)/shard_map/psum | solution.py:45
  157.3 2.2 multiply_add_fusion.1
  159.4 5.6 %stack.4 = f32[8,1536,256]{2,1,0:T(8,128)} broadcast(f32[1536,256]{1,0:T(8,128)S(1)} %multiply_add_fusion.1), dimensions={1,2} | broadcast | bytes 14155776 | tf_op jit(solution)/shard_map/stack | solution.py:53
  165.0 5.3 all-to-all-start
  170.7 138.6 %all-to-all-done = f32[8,1536,256]{2,1,0:T(8,128)} async-done(((f32[8,1536,256]{2,1,0:T(8,128)}), f32[8,1536,256]{2,1,0:T(8,128)}, u32[]{:S(2)}, u32[]{:S(2)}) %all-to-all-start) | async-done | bytes 12582944 | tf_op jit(solution)/shard_map/all_to_all | solution.py:53
  309.3 10.0 %copy.51 = bf16[8,1536,256]{1,2,0:T(8,128)(2,1)} copy(f32[8,1536,256]{2,1,0:T(8,128)} %all-to-all-done) | data formatting | bytes 18874368 | tf_op jit(solution)/shard_map/all_to_all | solution.py:53
  319.3 10.1 %fusion.39 = f32[1536,2048]{1,0:T(8,128)} fusion(bf16[1,32,2048]{2,1,0:T(8,128)(2,1)S(1)} %copy-done, f32[1536,32]{0,1:T(8,128)S(1)} %mul.170, bf16[1536,2048]{0,1:T(8,128)(2,1)} %bitcast.88, bf16[1,2048,32]{1,2,0:T(8,128)(2,1)S(1)} %copy-done.3), kind=kOutput, calls=%fused_computation.53 | convolution fusion | flops 403144704 | bytes 19333120 | tf_op jit(solution)/shard_map/dot_general | solution.py:108
  329.4 15.2 %copy.65 = f32[8,192,8,256]{3,2,0,1:T(8,128)} copy(f32[8,192,8,256]{3,2,1,0:T(8,128)} %bitcast.56) | data formatting | bytes 25165824 | tf_op jit(solution)/shard_map/reshape | solution.py:52
  344.6 75.1 %reduce-scatter.5.cloned.1.call-done = f32[1536,256]{1,0:T(8,128)} async-done(((f32[1536,2048]{1,0:T(8,128)}), f32[1536,256]{1,0:T(8,128)}) %reduce-scatter.5.cloned.1.call-update) | async-done | bytes 1572880 | tf_op jit(solution)/shard_map/reduce_scatter | solution.py:42
  419.8 1.7 multiply_reduce_fusion.1
  421.5 12.8 %psum.15 = f32[1536,1]{0,1:T(1,128)S(1)} all-reduce(f32[1536,1]{0,1:T(1,128)S(1)} %broadcast_in_dim.19), channel_id=1, replica_groups=mesh['group'=4,'member'=8] {'member'}, use_global_device_ids=true, to_apply=%region_8.9 | all-reduce | flops 1536 | bytes 12288 | tf_op jit(solution)/shard_map/psum | solution.py:45
  434.3 2.2 multiply_add_fusion
  436.9 74.9 %all_to_all.42 = bf16[8,1536,256]{2,1,0:T(8,128)(2,1)} all-to-all(bf16[8,1536,256]{2,1,0:T(8,128)(2,1)S(1)} %stack.5), channel_id=1, replica_groups=mesh['group'=4,'member'=8] {'member'}, dimensions={0} | all-to-all | bytes 12582912 | tf_op jit(solution)/shard_map/all_to_all | solution.py:53
  511.7 8.6 %copy.62 = bf16[8,1536,256]{1,2,0:T(8,128)(2,1)} copy(bf16[8,1536,256]{2,1,0:T(8,128)(2,1)} %all_to_all.42) | data formatting | bytes 12582912 | tf_op jit(solution)/shard_map/all_to_all | solution.py:53
  520.3 8.6 %copy.63 = bf16[1536,2048]{1,0:T(8,128)(2,1)} copy(bf16[1536,2048]{0,1:T(8,128)(2,1)} %bitcast.87) | data formatting | bytes 12582912 | tf_op jit(solution)/shard_map/convert_element_type | solution.py:110
  (46 shorter events, 3.8 us)
Async XLA Ops:
  6.5 312.8 %copy-start = (bf16[1,32,2048]{2,1,0:T(8,128)(2,1)S(1)}, bf16[1,32,2048]{2,1,0:T(8,128)(2,1)}, u32[]{:S(2)}) copy-start(bf16[1,32,2048]{2,1,0:T(8,128)(2,1)} %param.21) | copy-start | bytes 393220
  6.5 4.3 copy-start.4
  6.5 136.2 %reduce-scatter.3.cloned.1.call-start = ((), (), s32[]{:S(2)}) async-start(), calls=%async_computation.9 | async-start | bytes 14155776 | tf_op jit(solution)/shard_map/reduce_scatter | solution.py:42
  6.5 4.6 copy-start.1
  44.2 0.7 copy-start.2
  44.2 2.1 copy-start.6
  44.2 22.4 %copy-start.5 = (s32[192]{0:T(256)S(1)}, s32[192]{0:T(256)}, u32[]{:S(2)}) copy-start(s32[192]{0:T(256)} %param.13) | copy-start | bytes 2308
  103.0 12.2 %all-to-all-start.4 = ((bf16[4,8,12,256]{3,0,2,1:T(4,128)(2,1)}), bf16[4,8,12,256]{3,0,2,1:T(4,128)(2,1)S(1)}, u32[]{:S(2)}, u32[]{:S(2)}) async-start(bf16[4,8,12,256]{3,0,2,1:T(4,128)(2,1)} %copy.57), calls=%async_computation.5 | async-start | bytes 393216 | tf_op jit(solution)/shard_map/all_to_all | solution.py:85
  116.2 43.3 %all-to-all-start.5 = ((bf16[192,1,8,32]{0,3,1,2:T(8,128)(2,1)}), bf16[192,1,8,32]{0,3,1,2:T(8,128)(2,1)S(1)}, u32[]{:S(2)}, u32[]{:S(2)}) async-start(bf16[192,1,8,32]{0,3,1,2:T(8,128)(2,1)} %bitcast.46), calls=%async_computation.6 | async-start | bytes 262144 | tf_op jit(solution)/shard_map/all_to_all | solution.py:96
  165.0 144.3 %all-to-all-start = ((f32[8,1536,256]{2,1,0:T(8,128)}), f32[8,1536,256]{2,1,0:T(8,128)}, u32[]{:S(2)}, u32[]{:S(2)}) async-start(f32[8,1536,256]{2,1,0:T(8,128)} %stack.4), calls=%async_computation.1 | async-start | bytes 25165824 | tf_op jit(solution)/shard_map/all_to_all | solution.py:53
  170.3 249.4 %reduce-scatter.5.cloned.1.call-start = ((), (), s32[]{:S(2)}) async-start(), calls=%async_computation.10 | async-start | bytes 14155776 | tf_op jit(solution)/shard_map/reduce_scatter | solution.py:42
  170.7 148.6 %copy-start.3 = (bf16[1,2048,32]{1,2,0:T(8,128)(2,1)S(1)}, bf16[1,2048,32]{1,2,0:T(8,128)(2,1)}, u32[]{:S(2)}) copy-start(bf16[1,2048,32]{1,2,0:T(8,128)(2,1)} %param.20) | copy-start | bytes 393220
Sparse Core Ops, SparseCore 0:
  44.4 98.3 reduce-scatter.2
  329.5 90.2 reduce-scatter.4
